TPU v7x, 32 devices: a whole 2x2x4 slice. The times are simulated.
32 devices in a mesh: vec: 16 (over z, y, x), ao: 2 (over core).
Axes of the slice: x: 2, y: 2, z: 4, core: 2. Of those that a mesh axis runs over, the one named last changes fastest.
Arguments:
- cholesky: float32 [16, 1200, 1200], P('vec', 'ao'), may hold values from -6 to 6
- coefficients: float32 [2, 720000], P('ao', 'vec'), may hold values from -0.1875 to 0.1875
Outputs:
- mo_vectors: float32 [16, 128, 1072], P(None, 'vec', 'ao')
All inputs are finite; a program needn't handle non-finite values.
Results may differ from a plain program's by a relative error of at most 0.0001.
Values sent between devices are 32-bit elements; how exact they have to be, the bound alone decides.
A program may use at most 64 MiB of HBM per device.

v0:
```python
import functools

import jax
import jax.numpy as jnp
from jax import lax
from jax.experimental import pallas as pl
from jax.experimental.pallas import tpu as pltpu
from jax.sharding import PartitionSpec as P

NOCC = 128
LANES = 128
MESH = pl.DeviceIdType.MESH
F32 = jnp.float32
STEP, TURN = 24, 0


def up_to(size, step):
    return -(-size // step) * step


def simple_body(cholesky, coefficients):
    half_rows = cholesky.shape[1]
    own_flat = lax.all_gather(coefficients, "vec", axis=1, tiled=True)
    own_rows = own_flat.reshape(half_rows, own_flat.shape[1] // half_rows)
    occupied_own = own_rows[:, :NOCC]
    partial_x = jnp.einsum(
        "mi,pmn->pin",
        occupied_own,
        cholesky,
        precision=lax.Precision.HIGHEST,
        preferred_element_type=jnp.float32,
    )
    x_block = lax.psum_scatter(partial_x, "ao", scatter_dimension=2, tiled=True)
    virtual_own = own_rows[:, NOCC:]
    partial_y = jnp.einsum(
        "pin,na->pia",
        x_block,
        virtual_own,
        precision=lax.Precision.HIGHEST,
        preferred_element_type=jnp.float32,
    )
    summed = lax.psum_scatter(partial_y, "ao", scatter_dimension=2, tiled=True)
    owned = lax.all_to_all(summed, "vec", split_axis=1, concat_axis=0, tiled=True)
    return owned


def split(value):
    high = value.astype(jnp.bfloat16)
    return high, (value - high.astype(F32)).astype(jnp.bfloat16)


def product(left, right):
    (lh, ll), (rh, rl) = left, right
    dot = functools.partial(jnp.dot, preferred_element_type=F32)
    return dot(lh, rh) + (dot(lh, rl) + dot(ll, rh))


def kernel(
    n, starts, rows, pieces, plan, own_ref, l_ref, out_ref,
    rows_all, l_buf, occ_dense, vir_dense, x_full, x_out, x_in, x_send, x_recv, y_full, y_out, y_in,
    l_sem, occ_ss, occ_rs, vir_ss, vir_rs, x_ss, x_rs, pair_ss, pair_rs,
):
    me, core = lax.axis_index("vec"), lax.axis_index("ao")
    nz = n // 4
    x, y, z = me % 2, (me // 2) % 2, me // 4
    xp, yp, diag = me + 1 - 2 * x, me + 2 - 4 * y, me + 3 - 2 * x - 4 * y
    half, nao = l_ref.shape
    wide = vir_dense.shape[1]

    l_copy = pltpu.make_async_copy(l_ref, l_buf, l_sem)
    l_copy.start()
    rows_all[me, :, :own_ref.shape[1]] = own_ref[...]

    barrier = pltpu.get_barrier_semaphore()
    for d in range(1, n):
        pl.semaphore_signal(barrier, inc=1, device_id=((me + d) % n, core), device_id_type=MESH)
    pl.semaphore_signal(barrier, inc=1, device_id=(me, 1 - core), device_id_type=MESH)
    pl.semaphore_wait(barrier, n)

    def occ_copy(w, way, to):
        part = rows_all.at[w, :, pl.ds(0, NOCC)]
        return pltpu.make_async_remote_copy(
            src_ref=part, dst_ref=part, send_sem=occ_ss.at[way, to if way == 3 else w], recv_sem=occ_rs.at[w],
            device_id=(to, core), device_id_type=MESH)

    def vir_copy(p, w, way, to):
        part = rows_all.at[w, pl.ds(pieces[p][0], pieces[p][1]), pl.ds(NOCC, wide)]
        return pltpu.make_async_remote_copy(
            src_ref=part, dst_ref=part, send_sem=vir_ss.at[p, way, w], recv_sem=vir_rs.at[p, w],
            device_id=(to, core), device_id_type=MESH)

    def x_copy(w, to):
        return pltpu.make_async_remote_copy(
            src_ref=x_send.at[to], dst_ref=x_recv.at[w], send_sem=x_ss.at[to], recv_sem=x_rs.at[w],
            device_id=(to, core), device_id_type=MESH)

    def pair_copy(which, src, dst):
        return pltpu.make_async_remote_copy(
            src_ref=src, dst_ref=dst, send_sem=pair_ss.at[which], recv_sem=pair_rs.at[which],
            device_id=(me, 1 - core), device_id_type=MESH)

    def along(p, w, up=True, down=True):
        if up:
            pl.when(z < nz - 1)(lambda: vir_copy(p, w, 2, me + 4).start())
        if down:
            pl.when(z > 0)(lambda: vir_copy(p, w, 3, me - 4).start())

    def send_own(p):
        along(p, me)
        vir_copy(p, me, 0, xp).start()
        vir_copy(p, me, 1, yp).start()

    def line(k, p):
        if k >= nz:
            return
        for up in (True, False):
            @pl.when(z >= k if up else z + k < nz)
            def _():
                w = me - 4 * k if up else me + 4 * k
                vir_copy(p, w, 2, me).wait_recv()
                along(p, w, up, not up)
                vir_copy(p, w, 0, xp).start()
                vir_copy(p, w, 1, yp).start()

    def plane(k, p):
        def one(shift):
            wx, wy = xp + 4 * shift, yp + 4 * shift
            even = (z + shift) % 2 == 0
            cross = k == 0 or not pieces[p][2]
            vir_copy(p, wx, 0, me).wait_recv()
            if cross:
                pl.when(even)(lambda: vir_copy(p, wx, 1, yp).start())
            vir_copy(p, wy, 1, me).wait_recv()
            if cross:
                pl.when(jnp.logical_not(even))(lambda: vir_copy(p, wy, 0, xp).start())

        if k == 0:
            one(0)
        elif k < nz:
            pl.when(z >= k)(lambda: one(-k))
            pl.when(z + k < nz)(lambda: one(k))

    def corner(k, p):
        def one(shift, up, down):
            vir_copy(p, diag + 4 * shift, 0, me).wait_recv()
            if pieces[p][2]:
                along(p, diag + 4 * shift, up, down)

        if k == 0:
            one(0, True, True)
        elif k < nz:
            pl.when(z >= k)(lambda: one(-k, True, False))
            pl.when(z + k < nz)(lambda: one(k, False, True))

    first = core == 0
    state = {}

    def occ_spread(w):
        for way, to in enumerate((xp, yp, diag)):
            occ_copy(w, way, to).start()

    def occ_line():
        for d in range(1, nz):
            w = (me + 4 * d) % n
            occ_copy(w, 3, me).wait_recv()
            occ_spread(w)

    def occ_start():
        for d in range(1, nz):
            occ_copy(me, 3, (me + 4 * d) % n).start()
        occ_spread(me)
        occ_dense[...] = jnp.zeros_like(occ_dense)
        vir_dense[...] = jnp.zeros_like(vir_dense)
        x_full[...] = jnp.zeros_like(x_full)

    def half_transform():
        for d in range(nz):
            for other in (xp, yp, diag):
                occ_copy((other + 4 * d) % n, 3, me).wait_recv()
        for w in range(n):
            occ_dense[starts[w]:starts[w] + rows, :] += rows_all[w, :rows, :NOCC]
        l_copy.wait()
        occ_t = occ_dense[...].T[:, :half]
        x_full[:, :nao] = product(split(occ_t), split(l_buf[...]))
        whole = x_full[...]
        low = whole[:, :x_out.shape[1]]
        high = pltpu.roll(whole, x_full.shape[1] - half, 1)[:, :x_out.shape[1]]
        x_out[...] = jnp.where(first, high, low)
        state["own"] = jnp.where(first, low, high)
        pair_copy(0, x_out, x_in).start()

    def x_join():
        pair_copy(0, x_out, x_in).wait_recv()
        x_send[...] = (state["own"] + x_in[...]).reshape(x_send.shape)

    def x_start():
        for d in range(1, n):
            x_copy(me, (me + d) % n).start()
        x_recv[me] = x_send[me]

    def x_wait():
        for d in range(1, n):
            x_copy((me + d) % n, me).wait_recv()

    def join(w):
        vir_dense[starts[w]:starts[w] + rows, :] += rows_all[w, :rows, NOCC:]

    steps = dict(
        occ=occ_start, occline=occ_line, own=send_own, line=line, plane=plane, corner=corner,
        half=half_transform, xjoin=x_join, xstart=x_start, xwait=x_wait)
    for step, *args in plan:
        steps[step](*args)

    for w in range(n):
        join(w)
    y_full[...] = product(split(x_recv[...].reshape(x_out.shape)), split(vir_dense[...]))
    whole_y = y_full[...]
    low_y = whole_y[:, :y_out.shape[1]]
    high_y = pltpu.roll(whole_y, y_full.shape[1] - out_ref.shape[2], 1)[:, :y_out.shape[1]]
    y_out[...] = jnp.where(first, high_y, low_y)
    y_own = jnp.where(first, low_y, high_y)
    pair_copy(1, y_out, y_in).start()

    for d in range(1, n):
        x_copy(me, (me + d) % n).wait_send()
    for d in range(nz):
        for way in range(3):
            occ_copy((me + 4 * d) % n, way, xp).wait_send()
        if d:
            occ_copy(me, 3, (me + 4 * d) % n).wait_send()
    for p in range(len(pieces)):
        for zz in range(nz):
            w, wd = x + 2 * y + 4 * zz, diag + 4 * (zz - z)
            vir_copy(p, w, 0, xp).wait_send()
            vir_copy(p, w, 1, yp).wait_send()
            for slot in (w, wd) if pieces[p][2] else (w,):
                pl.when((z >= zz) & (z < nz - 1))(lambda: vir_copy(p, slot, 2, xp).wait_send())
                pl.when((z <= zz) & (z > 0))(lambda: vir_copy(p, slot, 3, xp).wait_send())
            crossed = (z == zz) if pieces[p][2] else (z >= 0)
            if zz % 2 == 0:
                pl.when(crossed)(lambda: vir_copy(p, xp + 4 * (zz - z), 1, yp).wait_send())
            else:
                pl.when(crossed)(lambda: vir_copy(p, yp + 4 * (zz - z), 0, xp).wait_send())
    pair_copy(0, x_out, x_in).wait_send()
    pair_copy(1, y_out, y_in).wait()
    out_ref[...] = (y_own + y_in[...])[:, :out_ref.shape[2]].reshape(out_ref.shape)


def plan_of(count, nz):
    every = range(count)

    def wave(name, k):
        return [(name, k, p) for p in every]

    plan = [("occ",), ("own", 0), ("occline",)] + [("own", p) for p in every[1:]]
    plan += wave("line", 1) + wave("plane", 0) + wave("line", 2) + [("half",)] + wave("plane", 1) + [("xjoin",)] + wave("line", 3) + [("xstart",)] + wave("corner", 0)
    plan += wave("plane", 2) + wave("corner", 1)
    for k in range(3, nz):
        plan += wave("line", k + 1) + wave("plane", k) + wave("corner", k - 1)
    return plan + wave("corner", nz - 1) + [("xwait",)]


def body(n, cholesky, coefficients):
    if cholesky.shape[0] != 1:
        return simple_body(cholesky, coefficients)
    half, nao = cholesky.shape[1:]
    per = coefficients.shape[1]
    nmo = per * n // half
    nvir = nmo - NOCC
    offsets = [w * per % nmo for w in range(n)]
    starts = tuple(w * per // nmo for w in range(n))
    rows = max(-(-(offset + per) // nmo) for offset in offsets)
    deep = up_to(rows, 8)
    me = lax.axis_index("vec")
    flat = coefficients[0]
    total = deep * nmo
    framed = jnp.zeros((total,), F32)
    for offset in sorted(set(offsets)):
        here = jnp.pad(flat, (offset, total - per - offset))
        framed = jnp.where(me * per % nmo == offset, here, framed)
    framed = framed.reshape(deep, nmo)
    wide = up_to(nvir, LANES)
    pieces = tuple((row, min(STEP, deep - row), row < TURN) for row in range(0, deep, STEP))
    plan = plan_of(len(pieces), n // 4)
    tall = up_to(max(half, starts[-1] + rows), LANES)
    part = up_to(nvir // 2, LANES)
    iblock = NOCC // n
    dma = pltpu.SemaphoreType.DMA
    vmem = pl.BlockSpec(memory_space=pltpu.VMEM)
    return pl.pallas_call(
        functools.partial(kernel, n, starts, rows, pieces, plan),
        out_shape=jax.ShapeDtypeStruct((n, iblock, nvir // 2), F32),
        in_specs=[vmem, pl.BlockSpec(memory_space=pl.ANY)],
        out_specs=vmem,
        scratch_shapes=[
            pltpu.VMEM((n, deep, NOCC + wide), F32),
            pltpu.VMEM((half, nao), F32),
            pltpu.VMEM((tall, NOCC), F32),
            pltpu.VMEM((tall, wide), F32),
            pltpu.VMEM((NOCC, up_to(nao, LANES)), F32),
            pltpu.VMEM((NOCC, tall), F32),
            pltpu.VMEM((NOCC, tall), F32),
            pltpu.VMEM((n, iblock, tall), F32),
            pltpu.VMEM((n, iblock, tall), F32),
            pltpu.VMEM((NOCC, wide), F32),
            pltpu.VMEM((NOCC, part), F32),
            pltpu.VMEM((NOCC, part), F32),
            dma, dma((4, n)), dma((n,)), dma((len(pieces), 4, n)), dma((len(pieces), n)), dma((n,)), dma((n,)), dma((2,)), dma((2,)),
        ],
        compiler_params=pltpu.CompilerParams(
            collective_id=0, has_side_effects=True, vmem_limit_bytes=60 * 1024 * 1024),
        name="transform",
    )(framed, cholesky[0])


def solution(mesh):
    n = mesh.shape["vec"]
    in_specs = (P("vec", "ao", None), P("ao", "vec"))
    out_specs = P(None, "vec", "ao")
    lines = n % 4 == 0 and mesh.shape["ao"] == 2 and NOCC % (8 * n) == 0
    step = functools.partial(body, n) if lines else simple_body
    return jax.shard_map(step, mesh=mesh, in_specs=in_specs, out_specs=out_specs, check_vma=False)
```

profile of v0, /device:TPU:1, one launch (start us, length us, event | category | flops | bytes accessed | tf_op | source)
XLA Modules:
  0.0 49.4 jit_solution(12427932316232675722)
XLA Ops:
  0.0 1.1 %select_select_fusion = f32[48000]{0:T(1024)S(1)} fusion(f32[45000]{0:T(1024)} %bitcast.3, pred[]{:T(512)S(6)} %eq.10, pred[]{:T(512)S(6)} %eq.9), kind=kLoop, calls=%fused_computation | loop fusion | flops 96000 | bytes 372002 | tf_op jit(solution)/shard_map/jit(_where)/select_n | solution.py:280
  1.1 0.9 %reshape.3.own_ref = f32[40,1200]{1,0:T(8,128)} reshape(f32[48000]{0:T(1024)S(1)} %select_select_fusion) | data formatting | bytes 384000 | tf_op jit(solution)/shard_map/reshape | solution.py:281
  2.0 45.7 %transform.1 = f32[16,8,536]{2,1,0:T(8,128)} custom-call(f32[40,1200]{1,0:T(8,128)} %reshape.3.own_ref, f32[600,1200]{1,0:T(8,128)} %bitcast.2), custom_call_target="tpu_custom_call" | custom-call | tf_op jit(solution)/shard_map/transform/pallas_call | solution.py:290
  47.6 1.7 %copy.4 = f32[16,8,536]{2,1,0:T(8,128)} copy(f32[16,8,536]{2,1,0:T(8,128)} %transform.1) | data formatting | bytes 548864
where the time goes:
time: 49.7 us; the launch traced here: 49.4 us
  Pallas kernels  45.7 us (92%)
  local copies, waits for them, and re-layouts  2.57 us (5%)
  other arithmetic  1.12 us (2%)
    pallas_call x1, Pallas kernels, body(): pl.pallas_call(functools.partial(kernel, n, starts, rows, pieces, plan),...  45.7 us
    unnamed x1, local copies, waits for them, and re-layouts  1.72 us
    select_n x1, other arithmetic, body(): framed = jnp.where(me * per % nmo == offset, here, framed)  1.12 us

commit v1 on v0

v1 whole, which is shorter than its diff:
```python
import functools
import math

import jax
import jax.numpy as jnp
from jax import lax
from jax.experimental import pallas as pl
from jax.experimental.pallas import tpu as pltpu
from jax.sharding import PartitionSpec as P

NOCC = 128
LANES = 128
MESH = pl.DeviceIdType.MESH
F32 = jnp.float32
BF16 = jnp.bfloat16


def up_to(size, step):
    return -(-size // step) * step


def simple_body(cholesky, coefficients):
    half_rows = cholesky.shape[1]
    own_flat = lax.all_gather(coefficients, "vec", axis=1, tiled=True)
    own_rows = own_flat.reshape(half_rows, own_flat.shape[1] // half_rows)
    occupied_own = own_rows[:, :NOCC]
    partial_x = jnp.einsum(
        "mi,pmn->pin",
        occupied_own,
        cholesky,
        precision=lax.Precision.HIGHEST,
        preferred_element_type=jnp.float32,
    )
    x_block = lax.psum_scatter(partial_x, "ao", scatter_dimension=2, tiled=True)
    virtual_own = own_rows[:, NOCC:]
    partial_y = jnp.einsum(
        "pin,na->pia",
        x_block,
        virtual_own,
        precision=lax.Precision.HIGHEST,
        preferred_element_type=jnp.float32,
    )
    summed = lax.psum_scatter(partial_y, "ao", scatter_dimension=2, tiled=True)
    owned = lax.all_to_all(summed, "vec", split_axis=1, concat_axis=0, tiled=True)
    return owned


def split(value):
    high = value.astype(BF16)
    return high, (value - high.astype(F32)).astype(BF16)


def product(left, right):
    (lh, ll), (rh, rl) = left, right
    dot = functools.partial(jnp.dot, preferred_element_type=F32)
    return dot(lh, rh) + (dot(lh, rl) + dot(ll, rh))


def tile_at(tiles, lane, offset):
    first, shift = divmod(offset, LANES)
    blank = jnp.zeros_like(tiles[0])
    here, after = (tiles[k] if 0 <= k < len(tiles) else blank for k in (first, first + 1))
    if shift == 0:
        return here
    turn = LANES - shift
    return jnp.where(lane < turn, pltpu.roll(here, turn, 1), pltpu.roll(after, turn, 1))


def kernel(
    n, starts, rows, deep, parts, sub_ref, l_ref, out_ref,
    sbuf, occ_all, vsend, va, l_buf, lh, ll, occ_dense, dense, vh, vl,
    x_out, x_in, x_own, x_send, x_recv, y_out, y_in, y_send, y_recv,
    l_sem, occ_zs, occ_ss, occ_rs, vx_ss, v_ss, v_rs, x_ss, xf_ss, x_rs, pair_ss, pair_rs, y_ss, y_rs, o_ss, o_rs,
):
    me, core = lax.axis_index("vec"), lax.axis_index("ao")
    nz = n // 4
    x, y, z = me % 2, (me // 2) % 2, me // 4
    xp, yp, diag = me + 1 - 2 * x, me + 2 - 4 * y, me + 3 - 2 * x - 4 * y
    half, nao = l_ref.shape
    subs, sub = sub_ref.shape
    wide = out_ref.shape[2]
    full = wide // LANES
    rest = wide - full * LANES
    groups = deep // 8
    body_rows = full * deep
    block = 2 * out_ref.shape[1]
    npair = n // 2
    mine = me // 2

    l_copy = pltpu.make_async_copy(l_ref, l_buf, l_sem)
    l_copy.start()

    barrier = pltpu.get_barrier_semaphore()
    for to in [(me + 4 * d) % n for d in range(1, nz)] + [xp, yp, diag]:
        pl.semaphore_signal(barrier, inc=1, device_id=(to, core), device_id_type=MESH)
    pl.semaphore_signal(barrier, inc=1, device_id=(me, 1 - core), device_id_type=MESH)

    sbuf[...] = jnp.zeros_like(sbuf)
    for t in range(sbuf.shape[0]):
        width = min(LANES, sub - t * LANES)
        sbuf[t, 8:8 + subs, :width] = sub_ref[:, t * LANES:t * LANES + width]
    lane = lax.broadcasted_iota(jnp.int32, (deep, LANES), 1)
    odd = (me * subs) % 2 == 1
    left, right = [], []
    for t in range(sbuf.shape[0]):
        before, even, after = (sbuf[t, pl.ds(8 + k, deep, stride=2), :] for k in (-1, 0, 1))
        left.append(jnp.where(odd, before, even))
        right.append(jnp.where(odd, even, after))
    columns = []
    for t in range(up_to(2 * sub, LANES) // LANES):
        value = tile_at(right, lane, t * LANES - sub)
        columns.append(value + left[t] if t < len(left) else value)
    occ_all[me] = columns[0]
    halves = [[tile_at(columns, lane, NOCC + h * wide + t * LANES) for t in range(full + 1)] for h in range(2)]
    tails = []
    for h in range(2):
        tail = jnp.zeros((8, LANES), F32)
        for g in range(groups):
            piece = jnp.where(lane[:8] < rest, halves[h][full][8 * g:8 * g + 8], 0)
            tail += pltpu.roll(piece, g * rest, 1) if g else piece
        tails.append(tail)
    for t in range(full):
        low, high = halves[0][t], halves[1][t]
        va[me, t * deep:(t + 1) * deep, :] = jnp.where(x == 0, low, high)
        vsend[t * deep:(t + 1) * deep, :] = jnp.where(x == 0, high, low)
    va[me, body_rows:body_rows + 8, :] = jnp.where(x == 0, tails[0], tails[1])
    vsend[body_rows:body_rows + 8, :] = jnp.where(x == 0, tails[1], tails[0])

    pl.semaphore_wait(barrier, nz + 3)

    def remote(src, dst, send_sem, recv_sem, to, on=core):
        return pltpu.make_async_remote_copy(
            src_ref=src, dst_ref=dst, send_sem=send_sem, recv_sem=recv_sem,
            device_id=(to, on), device_id_type=MESH)

    def occ_line_copy(w, d, to):
        return remote(occ_all.at[w], occ_all.at[w], occ_zs.at[d], occ_rs.at[w], to)

    def occ_copy(w, way, to):
        return remote(occ_all.at[w], occ_all.at[w], occ_ss.at[way, w], occ_rs.at[w], to)

    def half_copy(p, w, to):
        rng = pl.ds(parts[p][0], parts[p][1])
        return remote(vsend.at[rng], va.at[w, rng], vx_ss.at[p], v_rs.at[p, w], to)

    def vir_copy(p, w, way, to):
        ref = va.at[w, pl.ds(parts[p][0], parts[p][1])]
        return remote(ref, ref, v_ss.at[way, p, w], v_rs.at[p, w], to)

    def x_copy(q, w, d, to):
        return remote(x_send.at[q], x_recv.at[w], x_ss.at[d], x_rs.at[w], to)

    def x_pass(w, to):
        return remote(x_recv.at[w], x_recv.at[w], xf_ss.at[w], x_rs.at[w], to)

    def pair_copy():
        return remote(x_out, x_in, pair_ss, pair_rs, me, 1 - core)

    def y_copy(k, group):
        return remote(y_out.at[group], y_in.at[group], y_ss.at[k], y_rs.at[k], me, 1 - core)

    def o_copy(k, group):
        return remote(y_send.at[group], y_recv.at[group], o_ss.at[k], o_rs.at[k], xp, 1 - core)

    def signs(k, act):
        if 0 < k < nz:
            pl.when(z >= k)(lambda: act(-4 * k, True))
            pl.when(z + k < nz)(lambda: act(4 * k, False))

    def along(p, w, up=True, down=True):
        if up:
            pl.when(z < nz - 1)(lambda: vir_copy(p, w, 1, me + 4).start())
        if down:
            pl.when(z > 0)(lambda: vir_copy(p, w, 2, me - 4).start())

    def occ_spread(w):
        for way, to in enumerate((xp, yp, diag)):
            occ_copy(w, way, to).start()

    def occ_start():
        for d in range(1, nz):
            occ_line_copy(me, d, (me + 4 * d) % n).start()
        occ_spread(me)

    def occ_line():
        for k in range(1, nz):
            def act(offset, up):
                occ_copy(me + offset, 0, me).wait_recv()
                occ_spread(me + offset)
            signs(k, act)

    def own_start():
        for p in range(len(parts)):
            half_copy(p, me, xp).start()
            along(p, me)
            vir_copy(p, me, 0, yp).start()

    def prepare():
        dense[...] = jnp.zeros_like(dense)
        occ_dense[...] = jnp.zeros_like(occ_dense)
        edge = half // LANES * LANES
        lh[:, :, edge:] = jnp.zeros_like(lh[:, :, edge:])
        ll[:, :, edge:] = jnp.zeros_like(ll[:, :, edge:])
        l_copy.wait()
        for h in range(2):
            high, low = split(l_buf[:, h * half:(h + 1) * half])
            lh[h, :, :half] = high
            ll[h, :, :half] = low

    def cross(p):
        half_copy(p, xp, me).wait_recv()
        along(p, xp)
        vir_copy(p, xp, 0, yp).start()

    def line(k, p, column):
        def act(offset, up):
            w = (me if column == 0 else xp) + offset
            vir_copy(p, w, 1, me).wait_recv()
            along(p, w, up, not up)
            vir_copy(p, w, 0, yp).start()
        signs(k, act)

    def half_transform():
        for d in range(nz):
            for other in (xp, yp, diag):
                occ_copy((other + 4 * d) % n, 0, me).wait_recv()
        for w in range(n):
            occ_dense[starts[w]:starts[w] + rows, :] += occ_all[w, :rows, :]
        occ = split(occ_dense[...].T[:, :half])
        x_out[...] = product(occ, (lh[1 - core], ll[1 - core]))
        pair_copy().start()
        x_own[...] = product(occ, (lh[core], ll[core]))

    def x_start():
        pair_copy().wait_recv()
        x_send[...] = (x_own[...] + x_in[...]).reshape(x_send.shape)
        x_copy(mine, me, 0, xp).start()
        for d in range(1, npair):
            q = (mine + d) % npair
            x_copy(q, me, d, 2 * q + x).start()
        x_recv[me] = x_send[mine]

    def x_take(w):
        x_copy(mine, w, 0, me).wait_recv()
        x_pass(w, xp).start()

    def x_relay(k):
        if k == 0:
            x_take(yp)
        else:
            def act(offset, up):
                x_take(me + offset)
                x_take(yp + offset)
            signs(k, act)

    def y_wait():
        for p in range(len(parts)):
            for zz in range(nz):
                for other in (yp, diag):
                    vir_copy(p, (other + 4 * zz) % n, 0, me).wait_recv()

    def join():
        tlane = lane
        for w in range(n):
            top = starts[w]
            for t in range(full):
                dense[top:top + rows, t * LANES:(t + 1) * LANES] += va[w, t * deep:t * deep + rows, :]
            tail = va[w, body_rows:body_rows + 8, :]
            value = jnp.concatenate([pltpu.roll(tail, (LANES - g * rest) % LANES, 1) if g else tail for g in range(groups)], axis=0)
            value = jnp.where(tlane < rest, value, 0)
            dense[top:top + rows, full * LANES:(full + 1) * LANES] += value[:rows]
        high, low = split(dense[...])
        vh[...] = high
        vl[...] = low

    def plane_of(k):
        order = [sorted(range(nz), key=lambda other: (abs(other - zz), other)) for zz in range(nz)]
        which = 0
        for zz in range(nz):
            which = which + jnp.where(z == zz, order[zz][k], 0)
        return which

    far = core != x

    def chunk(k):
        plane = plane_of(k)
        group = pl.ds(4 * plane, 4)
        for j in range(4):
            w = 4 * plane + j

            @pl.when((w % 2 != x))
            def _():
                x_pass(w, me).wait_recv()
        tall = 4 * block
        value = product(split(x_recv[group].reshape(tall, x_recv.shape[2])), (vh[...], vl[...]))
        value = value.reshape(4, block, value.shape[1])
        low, high = value[:, :block // 2], value[:, block // 2:]
        y_out[group] = jnp.where(core == 0, high, low)
        y_send[group] = jnp.where(core == 0, low, high)
        y_copy(k, group).start()

    def finish(k):
        group = pl.ds(4 * plane_of(k), 4)
        y_copy(k, group).wait_recv()
        total = y_send[group] + y_in[group]
        y_send[group] = total

        @pl.when(far)
        def _():
            o_copy(k, group).start()

        @pl.when(jnp.logical_not(far))
        def _():
            out_ref[group] = total[:, :, :wide]

    def last(k):
        group = pl.ds(4 * plane_of(k), 4)

        @pl.when(far)
        def _():
            o_copy(k, group).wait_recv()
            out_ref[group] = y_recv[group, :, :wide]

    pieces = range(len(parts))
    occ_start()
    own_start()
    prepare()
    occ_line()
    for p in pieces:
        cross(p)
    for p in pieces:
        line(1, p, 0)
    half_transform()
    for p in pieces:
        line(1, p, 1)
    for p in pieces:
        line(2, p, 0)
    x_start()
    for p in pieces:
        line(2, p, 1)
    for k in range(3, nz):
        for column in range(2):
            for p in pieces:
                line(k, p, column)
    for k in range(nz):
        x_relay(k)
    y_wait()
    join()
    for k in range(nz):
        chunk(k)
        if k:
            finish(k - 1)
    finish(nz - 1)

    for d in range(1, nz):
        occ_line_copy(me, d, me).wait_send()
    for zz in range(nz):
        for way in range(3):
            occ_copy((me + 4 * zz) % n, way, xp).wait_send()
    for p in pieces:
        half_copy(p, me, xp).wait_send()
        for zz in range(nz):
            for base in (me, xp):
                w = base - 4 * z + 4 * zz
                vir_copy(p, w, 0, yp).wait_send()
                pl.when((z >= zz) & (z < nz - 1))(lambda: vir_copy(p, w, 1, yp).wait_send())
                pl.when((z <= zz) & (z > 0))(lambda: vir_copy(p, w, 2, yp).wait_send())
    pair_copy().wait_send()
    for d in range(npair):
        x_copy(mine, me, d, xp).wait_send()
    for d in range(1, npair):
        x_pass(((2 * (mine + d)) % n) + x, xp).wait_send()
    for k in range(nz):
        group = pl.ds(4 * plane_of(k), 4)
        y_copy(k, group).wait_send()
        pl.when(far)(lambda: o_copy(k, group).wait_send())
        last(k)


def body(n, cholesky, coefficients):
    half, nao = cholesky.shape[1:]
    per = coefficients.shape[1]
    nmo = per * n // half
    nvir = nmo - NOCC
    sub = math.gcd(per, nmo)
    wide = nvir // 2
    full, rest = wide // LANES, wide % LANES
    starts = tuple(w * per // nmo for w in range(n))
    rows = max(-(-(w * per % nmo + per) // nmo) for w in range(n))
    deep = up_to(rows, 8)
    if cholesky.shape[0] != 1 or nmo != 2 * sub or rest == 0 or rest * (deep // 8) > LANES:
        return simple_body(cholesky, coefficients)
    subs = per // sub
    tall = up_to(max(half, starts[-1] + rows), LANES)
    size = full * deep + 8
    cut = full // 2 * deep
    parts = ((0, cut), (cut, size - cut))
    iblock = NOCC // n
    spread = up_to(wide, LANES)
    nz = n // 4
    dma = pltpu.SemaphoreType.DMA
    vmem = pl.BlockSpec(memory_space=pltpu.VMEM)
    return pl.pallas_call(
        functools.partial(kernel, n, starts, rows, deep, parts),
        out_shape=jax.ShapeDtypeStruct((n, iblock, wide), F32),
        in_specs=[vmem, pl.BlockSpec(memory_space=pl.ANY)],
        out_specs=vmem,
        scratch_shapes=[
            pltpu.VMEM((up_to(sub, LANES) // LANES, up_to(9 + 2 * deep, 8), LANES), F32),
            pltpu.VMEM((n, deep, LANES), F32),
            pltpu.VMEM((size, LANES), F32),
            pltpu.VMEM((n, size, LANES), F32),
            pltpu.VMEM((half, nao), F32),
            pltpu.VMEM((2, half, tall), BF16),
            pltpu.VMEM((2, half, tall), BF16),
            pltpu.VMEM((tall, NOCC), F32),
            pltpu.VMEM((tall, spread), F32),
            pltpu.VMEM((tall, spread), BF16),
            pltpu.VMEM((tall, spread), BF16),
            pltpu.VMEM((NOCC, tall), F32),
            pltpu.VMEM((NOCC, tall), F32),
            pltpu.VMEM((NOCC, tall), F32),
            pltpu.VMEM((n // 2, 2 * iblock, tall), F32),
            pltpu.VMEM((n, 2 * iblock, tall), F32),
            pltpu.VMEM((n, iblock, spread), F32),
            pltpu.VMEM((n, iblock, spread), F32),
            pltpu.VMEM((n, iblock, spread), F32),
            pltpu.VMEM((n, iblock, spread), F32),
            dma, dma((nz,)), dma((3, n)), dma((n,)), dma((len(parts),)), dma((3, len(parts), n)), dma((len(parts), n)),
            dma((n // 2,)), dma((n,)), dma((n,)), dma, dma, dma((nz,)), dma((nz,)), dma((nz,)), dma((nz,)),
        ],
        compiler_params=pltpu.CompilerParams(
            collective_id=0, has_side_effects=True, vmem_limit_bytes=32 * 1024 * 1024),
        name="transform",
    )(coefficients[0].reshape(subs, sub), cholesky[0])


def solution(mesh):
    n = mesh.shape["vec"]
    in_specs = (P("vec", "ao", None), P("ao", "vec"))
    out_specs = P(None, "vec", "ao")
    lines = n % 4 == 0 and mesh.shape["ao"] == 2 and NOCC % (8 * n) == 0
    step = functools.partial(body, n) if lines else simple_body
    return jax.shard_map(step, mesh=mesh, in_specs=in_specs, out_specs=out_specs, check_vma=False)
```

time: 49.7 us -> 45.3 us (0.911)
  Pallas kernels: 45.7 us -> 39.8 us
  other arithmetic: 1.12 us -> 2 us
  local copies, waits for them, and re-layouts: 2.57 us -> 3.27 us
    pallas_call x1, Pallas kernels: 45.7 us -> 39.8 us  [body(): pl.pallas_call(functools.partial(kernel, n, starts, rows, deep, parts), o...]
    unnamed x0 -> x1, other arithmetic: none -> 2 us
    unnamed x1 -> x4, local copies, waits for them, and re-layouts: 1.72 us -> 3.1 us
    select_n x1 -> x0, other arithmetic: 1.12 us -> none  [body(): framed = jnp.where(me * per % nmo == offset, here, framed)]
    reshape x1 -> x0, local copies, waits for them, and re-layouts: 0.85 us -> none  [body(): framed = framed.reshape(deep, nmo)]
where the time goes in v1:
time: 45.3 us; the launch traced here: 45.1 us
  Pallas kernels  39.8 us (88%)
  local copies, waits for them, and re-layouts  3.27 us (7%)
  other arithmetic  2 us (4%)
    pallas_call x1, Pallas kernels, body(): pl.pallas_call(functools.partial(kernel, n, starts, rows, deep, parts), o...  39.8 us
    unnamed x4, local copies, waits for them, and re-layouts  3.1 us
    unnamed x1, other arithmetic  2 us

profile of v1, /device:TPU:1, one launch (start us, length us, event | category | flops | bytes accessed | tf_op | source)
XLA Modules:
  0.0 45.1 jit_solution(5747447263982044100)
XLA Ops:
  0.0 0.5 %broadcast.3 = f32[]{:T(128)} broadcast(f32[]{:T(128)} %constant.5), dimensions={} | broadcast | bytes 8 | tf_op args[1]
  0.5 2.0 %reduce.3 = f32[45000]{0:T(1024)S(1)} reduce(f32[1,45000]{1,0:T(1,128)} %param.3, f32[]{:T(128)} %broadcast.3), dimensions={0}, to_apply=%param.3.reduce_sub_computation.3 | reduce | bytes 360004 | tf_op args[1]
  2.5 0.2 reshape_squeeze.3.sub_ref
  2.7 0.0 copy-start
  2.7 1.9 %copy-done = f32[1,600,1200]{2,1,0:T(8,128)S(1)} copy-done((f32[1,600,1200]{2,1,0:T(8,128)S(1)}, f32[1,600,1200]{2,1,0:T(8,128)}, u32[]{:S(2)}) %copy-start) | copy-done | bytes 2880024
  4.6 39.8 %transform.1 = f32[16,8,536]{2,1,0:T(8,128)S(1)} custom-call(f32[75,600]{1,0:T(8,128)S(1)} %reshape_squeeze.3.sub_ref, f32[600,1200]{1,0:T(8,128)S(1)} %bitcast.1), custom_call_target="tpu_custom_call" | custom-call | tf_op jit(solution)/shard_map/transform/pallas_call | solution.py:403
  44.4 0.7 %copy.4 = f32[16,8,536]{2,1,0:T(8,128)} copy(f32[16,8,536]{2,1,0:T(8,128)S(1)} %transform.1) | data formatting | bytes 548864
Async XLA Ops:
  2.7 1.9 %copy-start = (f32[1,600,1200]{2,1,0:T(8,128)S(1)}, f32[1,600,1200]{2,1,0:T(8,128)}, u32[]{:S(2)}) copy-start(f32[1,600,1200]{2,1,0:T(8,128)} %param.2) | copy-start | bytes 8640004

commit v2 on v1

v2 whole, which is shorter than its diff:
```python
import functools
import math

import jax
import jax.numpy as jnp
from jax import lax
from jax.experimental import pallas as pl
from jax.experimental.pallas import tpu as pltpu
from jax.sharding import PartitionSpec as P

NOCC = 128
LANES = 128
MESH = pl.DeviceIdType.MESH
F32 = jnp.float32
TURN, TURNED, GROUPS = 1, (1,), 4
BF16 = jnp.bfloat16


def up_to(size, step):
    return -(-size // step) * step


def simple_body(cholesky, coefficients):
    half_rows = cholesky.shape[1]
    own_flat = lax.all_gather(coefficients, "vec", axis=1, tiled=True)
    own_rows = own_flat.reshape(half_rows, own_flat.shape[1] // half_rows)
    occupied_own = own_rows[:, :NOCC]
    partial_x = jnp.einsum(
        "mi,pmn->pin",
        occupied_own,
        cholesky,
        precision=lax.Precision.HIGHEST,
        preferred_element_type=jnp.float32,
    )
    x_block = lax.psum_scatter(partial_x, "ao", scatter_dimension=2, tiled=True)
    virtual_own = own_rows[:, NOCC:]
    partial_y = jnp.einsum(
        "pin,na->pia",
        x_block,
        virtual_own,
        precision=lax.Precision.HIGHEST,
        preferred_element_type=jnp.float32,
    )
    summed = lax.psum_scatter(partial_y, "ao", scatter_dimension=2, tiled=True)
    owned = lax.all_to_all(summed, "vec", split_axis=1, concat_axis=0, tiled=True)
    return owned


def split(value):
    high = value.astype(BF16)
    return high, (value - high.astype(F32)).astype(BF16)


def product(left, right):
    (lh, ll), (rh, rl) = left, right
    dot = functools.partial(jnp.dot, preferred_element_type=F32)
    return dot(lh, rh) + (dot(lh, rl) + dot(ll, rh))


def tile_at(tiles, lane, offset):
    first, shift = divmod(offset, LANES)
    blank = jnp.zeros_like(tiles[0])
    here, after = (tiles[k] if 0 <= k < len(tiles) else blank for k in (first, first + 1))
    if shift == 0:
        return here
    turn = LANES - shift
    return jnp.where(lane < turn, pltpu.roll(here, turn, 1), pltpu.roll(after, turn, 1))


def kernel(
    n, starts, rows, deep, sub, parts, split_at, raw_ref, l_ref, out_ref,
    flat, sbuf, occ_all, vsend, va, l_buf, lh, ll, occ_dense, oh, ol, dense, vh, vl,
    x_out, x_in, x_own, x_send, x_recv, y_out, y_in, y_sum, y_recv,
    l_sem, occ_zs, occ_ss, occ_rs, vx_ss, v_ss, v_rs, x_ss, xf_ss, x_rs, pair_ss, pair_rs, y_ss, y_rs, o_ss, o_rs,
):
    me, core = lax.axis_index("vec"), lax.axis_index("ao")
    nz = n // 4
    x, y, z = me % 2, (me // 2) % 2, me // 4
    xp, yp, diag = me + 1 - 2 * x, me + 2 - 4 * y, me + 3 - 2 * x - 4 * y
    half, nao = l_ref.shape
    per = raw_ref.shape[1]
    subs = per // sub
    wide = out_ref.shape[2]
    full = wide // LANES
    rest = wide - full * LANES
    groups = deep // 8
    body_rows = full * rows
    block = 2 * out_ref.shape[1]
    npair = n // 2
    mine = me // 2

    l_copy = pltpu.make_async_copy(l_ref, l_buf, l_sem)
    l_copy.start()

    barrier = pltpu.get_barrier_semaphore()
    for to in [(me + 4 * d) % n for d in range(1, nz)] + [xp, yp, diag]:
        pl.semaphore_signal(barrier, inc=1, device_id=(to, core), device_id_type=MESH)
    pl.semaphore_signal(barrier, inc=1, device_id=(me, 1 - core), device_id_type=MESH)

    sbuf[...] = jnp.zeros_like(sbuf)
    for k in range(up_to(per, LANES) // LANES):
        width = min(LANES, per - k * LANES)
        flat[k:k + 1, :width] = raw_ref[:, k * LANES:k * LANES + width]
    period = LANES // math.gcd(sub, LANES)
    step = period * sub // LANES
    lane = lax.broadcasted_iota(jnp.int32, (deep, LANES), 1)
    for b in range(min(period, subs)):
        count = -(-(subs - b) // period)
        for t in range(sbuf.shape[0]):
            at, shift = divmod(b * sub + t * LANES, LANES)
            value = flat[pl.ds(at, count, stride=step), :]
            if shift:
                later = flat[pl.ds(at + 1, count, stride=step), :]
                turn = LANES - shift
                value = jnp.where(lane[:count] < turn, pltpu.roll(value, turn, 1), pltpu.roll(later, turn, 1))
            value = jnp.where(lane[:count] < sub - t * LANES, value, 0)
            sbuf[t, pl.ds(8 + b, count, stride=period), :] = value
    odd = (me * subs) % 2 == 1
    left, right = [], []
    for t in range(sbuf.shape[0]):
        before, even, after = (sbuf[t, pl.ds(8 + k, deep, stride=2), :] for k in (-1, 0, 1))
        left.append(jnp.where(odd, before, even))
        right.append(jnp.where(odd, even, after))
    columns = []
    for t in range(up_to(2 * sub, LANES) // LANES):
        value = tile_at(right, lane, t * LANES - sub)
        columns.append(value + left[t] if t < len(left) else value)
    occ_all[me] = columns[0]
    halves = [[tile_at(columns, lane, NOCC + h * wide + t * LANES) for t in range(full + 1)] for h in range(2)]
    tails = []
    for h in range(2):
        tail = jnp.zeros((8, LANES), F32)
        for g in range(groups):
            piece = jnp.where(lane[:8] < rest, halves[h][full][8 * g:8 * g + 8], 0)
            tail += pltpu.roll(piece, g * rest, 1) if g else piece
        tails.append(tail)
    for t in range(full):
        low, high = halves[0][t], halves[1][t]
        va[me, t * rows:(t + 1) * rows, :] = jnp.where(x == 0, low, high)[:rows]
        vsend[t * rows:(t + 1) * rows, :] = jnp.where(x == 0, high, low)[:rows]
    va[me, body_rows:body_rows + 8, :] = jnp.where(x == 0, tails[0], tails[1])
    vsend[body_rows:body_rows + 8, :] = jnp.where(x == 0, tails[1], tails[0])

    pl.semaphore_wait(barrier, nz + 3)

    def remote(src, dst, send_sem, recv_sem, to, on=core):
        return pltpu.make_async_remote_copy(
            src_ref=src, dst_ref=dst, send_sem=send_sem, recv_sem=recv_sem,
            device_id=(to, on), device_id_type=MESH)

    def occ_line_copy(w, d, to):
        return remote(occ_all.at[w], occ_all.at[w], occ_zs.at[d], occ_rs.at[w], to)

    def occ_copy(w, way, to):
        return remote(occ_all.at[w], occ_all.at[w], occ_ss.at[way, w], occ_rs.at[w], to)

    def half_copy(p, w, to):
        rng = pl.ds(parts[p][0], parts[p][1])
        return remote(vsend.at[rng], va.at[w, rng], vx_ss.at[p], v_rs.at[p, w], to)

    def vir_copy(p, w, way, to):
        ref = va.at[w, pl.ds(parts[p][0], parts[p][1])]
        return remote(ref, ref, v_ss.at[way, p, w], v_rs.at[p, w], to)

    def x_copy(q, w, d, to):
        return remote(x_send.at[q], x_recv.at[w], x_ss.at[d], x_rs.at[w], to)

    def x_pass(w, to):
        return remote(x_recv.at[w], x_recv.at[w], xf_ss.at[w], x_rs.at[w], to)

    def pair_copy():
        return remote(x_out, x_in, pair_ss, pair_rs, me, 1 - core)

    def y_copy(w):
        return remote(y_out.at[w], y_in.at[w], y_ss.at[w], y_rs.at[w], me, 1 - core)

    def o_copy(w):
        return remote(y_sum.at[w], y_recv.at[w], o_ss.at[w], o_rs.at[w], xp, 1 - core)

    state = dict(end=False)

    def start(copy):
        copy.wait_send() if state["end"] else copy.start()

    def recv(copy, *where):
        if not state["end"]:
            copy(*where).wait_recv()

    def signs(k, act):
        if 0 < k < nz:
            pl.when(z >= k)(lambda: act(-4 * k, True))
            pl.when(z + k < nz)(lambda: act(4 * k, False))

    def along(p, w, up=True, down=True):
        if up:
            pl.when(z < nz - 1)(lambda: start(vir_copy(p, w, 1, me + 4)))
        if down:
            pl.when(z > 0)(lambda: start(vir_copy(p, w, 2, me - 4)))

    def occ_spread(w):
        for way, to in enumerate((xp, yp, diag)):
            start(occ_copy(w, way, to))

    def occ_start():
        for d in range(1, nz):
            start(occ_line_copy(me, d, (me + 4 * d) % n))
        occ_spread(me)

    def occ_line():
        for k in range(1, nz):
            def act(offset, up):
                recv(occ_copy, me + offset, 0, me)
                occ_spread(me + offset)
            signs(k, act)

    def own_start(p):
        start(half_copy(p, me, xp))
        along(p, me)
        start(vir_copy(p, me, 0, yp))

    def prepare():
        dense[...] = jnp.zeros_like(dense)
        occ_dense[...] = jnp.zeros_like(occ_dense)
        edge = half // LANES * LANES
        lh[:, :, edge:] = jnp.zeros_like(lh[:, :, edge:])
        ll[:, :, edge:] = jnp.zeros_like(ll[:, :, edge:])
        l_copy.wait()
        for h in range(2):
            high, low = split(l_buf[:, h * half:(h + 1) * half])
            lh[h, :, :half] = high
            ll[h, :, :half] = low

    def cross(p):
        recv(half_copy, p, xp, me)
        along(p, xp)
        start(vir_copy(p, xp, 0, yp))

    def line(k, p, column, on=True, over=True):
        turned = p in TURNED and column == 0 and k <= TURN

        def act(offset, up):
            w = (me if column == 0 else xp) + offset
            if on:
                recv(vir_copy, p, w, 1, me)
                along(p, w, up, not up)
            if over and not turned:
                start(vir_copy(p, w, 0, yp))
        signs(k, act)

    def turn(k, p):
        if p not in TURNED or not TURN or k > TURN:
            return
        if k == 0:
            recv(vir_copy, p, yp, 0, me)
            along(p, yp)

        def act(offset, up):
            recv(vir_copy, p, yp + offset, 1, me)
            if k < TURN:
                along(p, yp + offset, up, not up)
        signs(k, act)

    def occ_wait():
        for d in range(nz):
            for other in (xp, yp, diag):
                occ_copy((other + 4 * d) % n, 0, me).wait_recv()

    def occ_join():
        for w in range(n):
            occ_dense[starts[w]:starts[w] + rows, :] += occ_all[w, :rows, :]
        oh[...], ol[...] = split(occ_dense[...].T[:, :half])

    def x_other():
        x_out[...] = product((oh[...], ol[...]), (lh[1 - core], ll[1 - core]))
        pair_copy().start()

    def x_mine():
        x_own[...] = product((oh[...], ol[...]), (lh[core], ll[core]))

    def x_start():
        pair_copy().wait_recv()
        x_send[...] = (x_own[...] + x_in[...]).reshape(x_send.shape)
        x_copy(mine, me, 0, xp).start()
        for d in range(1, npair):
            q = (mine + d) % npair
            x_copy(q, me, d, 2 * q + x).start()
        x_recv[me] = x_send[mine]

    def x_take(w):
        x_copy(mine, w, 0, me).wait_recv()
        x_pass(w, xp).start()

    orders = [sorted(range(nz), key=lambda other: (abs(other - zz), other)) for zz in range(nz)]

    def near(base, k):
        plane = 0
        for zz in range(nz):
            plane = plane + jnp.where(z == zz, orders[zz][k], 0)
        return base + 4 * (plane - z)

    def turns(line_base, other_base):
        order = sorted([(k, 0, line_base) for k in range(nz)] + [(k + 1.5, 1, other_base) for k in range(nz)], key=lambda e: e[:2])
        return [near(base, int(k - 1.5 * side)) for k, side, base in order]

    def x_relay(count):
        for w in relays[count[0]:count[1]]:
            x_take(w)

    relays = turns(me, yp)[1:]
    groups_of = [turns(me, yp)]
    passed = turns(xp, diag)
    groups_of += [passed[k:k + split_at] for k in range(0, len(passed), split_at)]

    def y_wait(p):
        for other in (yp, diag):
            first = TURN + 1 if p in TURNED and other is yp and TURN else 0
            if first == 0:
                recv(vir_copy, p, other, 0, me)
            for k in range(max(first, 1), nz):
                signs(k, lambda offset, up: recv(vir_copy, p, other + offset, 0, me))

    def join(w):
        top = starts[w]
        for t in range(full):
            dense[top:top + rows, t * LANES:(t + 1) * LANES] += va[w, t * rows:(t + 1) * rows, :]
        tail = va[w, body_rows:body_rows + 8, :]
        value = jnp.concatenate([pltpu.roll(tail, (LANES - g * rest) % LANES, 1) if g else tail for g in range(groups)], axis=0)
        value = jnp.where(lane < rest, value, 0)
        dense[top:top + rows, full * LANES:(full + 1) * LANES] += value[:rows]

    def join_side(mine_side):
        for yy in range(2):
            @pl.when((y == yy) == mine_side)
            def _():
                for w in range(n):
                    if (w // 2) % 2 == yy:
                        join(w)

    far = core != x

    def ready():
        high, low = split(dense[...])
        vh[...] = high
        vl[...] = low

    def chunk(g):
        group = groups_of[g]
        for w in group:
            if g:
                x_pass(w, me).wait_recv()
        rows_x = jnp.concatenate([x_recv[w] for w in group], axis=0)
        value = product(split(rows_x), (vh[...], vl[...]))
        for j, w in enumerate(group):
            low = value[j * block:j * block + block // 2]
            high = value[j * block + block // 2:(j + 1) * block]
            y_out[w] = jnp.where(core == 0, high, low)
            y_sum[w] = jnp.where(core == 0, low, high)
        for w in group:
            y_copy(w).start()

    def finish(g):
        for w in groups_of[g]:
            y_copy(w).wait_recv()
            total = y_sum[w] + y_in[w]
            y_sum[w] = total

            @pl.when(jnp.logical_not(far))
            def _():
                out_ref[w] = total[:, :wide]
        for w in groups_of[g]:
            pl.when(far)(lambda: o_copy(w).start())

    def last(g):
        for w in groups_of[g]:
            @pl.when(far)
            def _():
                o_copy(w).wait_recv()
                out_ref[w] = y_recv[w, :, :wide]

    pieces = range(len(parts))
    occ_start()
    for p in pieces:
        own_start(p)
    prepare()
    occ_line()
    for p in pieces:
        cross(p)
    for p in pieces:
        line(1, p, 0)
    for p in pieces:
        turn(0, p)
    occ_wait()
    occ_join()
    x_other()
    x_mine()
    for p in pieces:
        line(1, p, 1, over=False)
    for p in pieces:
        line(2, p, 0, over=False)
    x_start()
    for p in pieces:
        line(1, p, 1, on=False)
    for p in pieces:
        line(2, p, 0, on=False)
    for p in pieces:
        turn(1, p)
    for p in pieces:
        line(2, p, 1)
    x_relay((0, 1))
    for p in pieces:
        line(3, p, 0)
    for p in pieces:
        turn(2, p)
    x_relay((1, 2))
    for p in pieces:
        line(3, p, 1)
    for p in pieces:
        turn(3, p)
    x_relay((2, 2 * nz - 1))
    join_side(True)
    for p in pieces:
        y_wait(p)
    join_side(False)
    ready()
    chunk(0)
    for g in range(1, len(groups_of)):
        chunk(g)
        finish(g - 1)
    finish(len(groups_of) - 1)

    state["end"] = True
    occ_start()
    occ_line()
    for p in pieces:
        own_start(p)
        cross(p)
        for k in range(nz):
            line(k, p, 0)
            line(k, p, 1)
            turn(k, p)
    pair_copy().wait_send()
    for d in range(npair):
        x_copy(mine, me, d, xp).wait_send()
    for d in range(1, npair):
        x_pass(((2 * (mine + d)) % n) + x, xp).wait_send()
    for w in range(n):
        y_copy(w).wait_send()
        pl.when(far)(lambda: o_copy(w).wait_send())
    for g in list(range(1, len(groups_of))) + [0]:
        last(g)


def body(n, cholesky, coefficients):
    half, nao = cholesky.shape[1:]
    per = coefficients.shape[1]
    nmo = per * n // half
    nvir = nmo - NOCC
    sub = math.gcd(per, nmo)
    wide = nvir // 2
    full, rest = wide // LANES, wide % LANES
    starts = tuple(w * per // nmo for w in range(n))
    rows = max(-(-(w * per % nmo + per) // nmo) for w in range(n))
    deep = up_to(rows, 8)
    if cholesky.shape[0] != 1 or nmo != 2 * sub or rest == 0 or rest * (deep // 8) > LANES:
        return simple_body(cholesky, coefficients)
    tall = up_to(max(half, starts[-1] + rows), LANES)
    size = up_to(full * rows + 8, 8)
    cut = size // 16 * 8
    parts = ((0, cut), (cut, size - cut))
    iblock = NOCC // n
    spread = up_to(wide, LANES)
    nz = n // 4
    dma = pltpu.SemaphoreType.DMA
    vmem = pl.BlockSpec(memory_space=pltpu.VMEM)
    return pl.pallas_call(
        functools.partial(kernel, n, starts, rows, deep, sub, parts, GROUPS),
        out_shape=jax.ShapeDtypeStruct((n, iblock, wide), F32),
        in_specs=[vmem, pl.BlockSpec(memory_space=pl.ANY)],
        out_specs=vmem,
        scratch_shapes=[
            pltpu.VMEM((up_to(per // LANES + 2, 8), LANES), F32),
            pltpu.VMEM((up_to(sub, LANES) // LANES, up_to(9 + 2 * deep, 8), LANES), F32),
            pltpu.VMEM((n, deep, LANES), F32),
            pltpu.VMEM((size, LANES), F32),
            pltpu.VMEM((n, size, LANES), F32),
            pltpu.VMEM((half, nao), F32),
            pltpu.VMEM((2, half, tall), BF16),
            pltpu.VMEM((2, half, tall), BF16),
            pltpu.VMEM((tall, NOCC), F32),
            pltpu.VMEM((NOCC, half), BF16),
            pltpu.VMEM((NOCC, half), BF16),
            pltpu.VMEM((tall, spread), F32),
            pltpu.VMEM((tall, spread), BF16),
            pltpu.VMEM((tall, spread), BF16),
            pltpu.VMEM((NOCC, tall), F32),
            pltpu.VMEM((NOCC, tall), F32),
            pltpu.VMEM((NOCC, tall), F32),
            pltpu.VMEM((n // 2, 2 * iblock, tall), F32),
            pltpu.VMEM((n, 2 * iblock, tall), F32),
            *[pltpu.VMEM((n, iblock, spread), F32)] * 4,
            dma, dma((nz,)), dma((3, n)), dma((n,)), dma((len(parts),)), dma((3, len(parts), n)), dma((len(parts), n)),
            dma((n // 2,)), dma((n,)), dma((n,)), dma, dma, *[dma((n,))] * 4,
        ],
        compiler_params=pltpu.CompilerParams(
            collective_id=0, has_side_effects=True, vmem_limit_bytes=53 * 1024 * 1024),
        name="transform",
    )(coefficients, cholesky.reshape(half, nao))


def solution(mesh):
    n = mesh.shape["vec"]
    in_specs = (P("vec", "ao", None), P("ao", "vec"))
    out_specs = P(None, "vec", "ao")
    lines = n % 4 == 0 and mesh.shape["ao"] == 2 and NOCC % (8 * n) == 0
    step = functools.partial(body, n) if lines else simple_body
    return jax.shard_map(step, mesh=mesh, in_specs=in_specs, out_specs=out_specs, check_vma=False)
```

time: 45.3 us -> 40.9 us (0.903)
  other arithmetic: 2 us -> 0 us
  local copies, waits for them, and re-layouts: 3.27 us -> 1.65 us
  Pallas kernels: 39.8 us -> 39.1 us
    unnamed x1 -> x0, other arithmetic: 2 us -> none
    unnamed x4 -> x3, local copies, waits for them, and re-layouts: 3.1 us -> 1.65 us
    pallas_call x1, Pallas kernels: 39.8 us -> 39.1 us  [body(): pl.pallas_call(functools.partial(kernel, n, starts, rows, deep, sub, part...]
where the time goes in v2:
time: 40.9 us; the launch traced here: 40.8 us
  Pallas kernels  39.1 us (96%)
  local copies, waits for them, and re-layouts  1.65 us (4%)
    pallas_call x1, Pallas kernels, body(): pl.pallas_call(functools.partial(kernel, n, starts, rows, deep, sub, part...  39.1 us
    unnamed x3, local copies, waits for them, and re-layouts  1.65 us

profile of v2, /device:TPU:1, one launch (start us, length us, event | category | flops | bytes accessed | tf_op | source)
XLA Modules:
  0.0 40.8 jit_solution(6556582316303180599)
XLA Ops:
  0.0 0.0 copy-start
  0.0 0.9 %copy-done = f32[1,45000]{1,0:T(1,128)S(1)} copy-done((f32[1,45000]{1,0:T(1,128)S(1)}, f32[1,45000]{1,0:T(1,128)}, u32[]{:S(2)}) %copy-start) | copy-done | bytes 180024
  0.9 39.1 %transform.1 = f32[16,8,536]{2,1,0:T(8,128)S(1)} custom-call(f32[1,45000]{1,0:T(1,128)S(1)} %copy-done, f32[600,1200]{1,0:T(8,128)} %bitcast.1), custom_call_target="tpu_custom_call" | custom-call | tf_op jit(solution)/shard_map/transform/pallas_call | solution.py:475
  40.1 0.7 %copy.4 = f32[16,8,536]{2,1,0:T(8,128)} copy(f32[16,8,536]{2,1,0:T(8,128)S(1)} %transform.1) | data formatting | bytes 548864
Async XLA Ops:
  0.0 0.9 %copy-start = (f32[1,45000]{1,0:T(1,128)S(1)}, f32[1,45000]{1,0:T(1,128)}, u32[]{:S(2)}) copy-start(f32[1,45000]{1,0:T(1,128)} %raw_ref.1) | copy-start | bytes 540004

commit v3 on v2

--- a/solution.py
+++ b/solution.py
@@ -70,8 +70,8 @@
 def kernel(
     n, starts, rows, deep, sub, parts, split_at, raw_ref, l_ref, out_ref,
     flat, sbuf, occ_all, vsend, va, l_buf, lh, ll, occ_dense, oh, ol, dense, vh, vl,
-    x_out, x_in, x_own, x_send, x_recv, y_out, y_in, y_sum, y_recv,
-    l_sem, occ_zs, occ_ss, occ_rs, vx_ss, v_ss, v_rs, x_ss, xf_ss, x_rs, pair_ss, pair_rs, y_ss, y_rs, o_ss, o_rs,
+    x_out, x_in, x_own, x_send, x_recv, y_out, y_in, y_sum, y_recv, t_out, t_in,
+    l_sem, occ_zs, occ_ss, occ_rs, vx_ss, v_ss, v_rs, x_ss, xf_ss, x_rs, pair_ss, pair_rs, y_ss, y_rs, o_ss, o_rs, t_ss, t_rs,
 ):
     me, core = lax.axis_index("vec"), lax.axis_index("ao")
     nz = n // 4
@@ -175,7 +175,11 @@
         return remote(y_out.at[w], y_in.at[w], y_ss.at[w], y_rs.at[w], me, 1 - core)
 
     def o_copy(w):
-        return remote(y_sum.at[w], y_recv.at[w], o_ss.at[w], o_rs.at[w], xp, 1 - core)
+        main = pl.ds(0, full * LANES)
+        return remote(y_sum.at[w, :, main], y_recv.at[w, :, main], o_ss.at[w], o_rs.at[w], xp, 1 - core)
+
+    def t_copy(slot):
+        return remote(t_out.at[slot], t_in.at[slot], t_ss.at[slot], t_rs.at[slot], xp, 1 - core)
 
     state = dict(end=False)
 
@@ -260,10 +264,11 @@
                 along(p, yp + offset, up, not up)
         signs(k, act)
 
-    def occ_wait():
-        for d in range(nz):
-            for other in (xp, yp, diag):
-                occ_copy((other + 4 * d) % n, 0, me).wait_recv()
+    def occ_wait(k):
+        for other in (xp, yp, diag):
+            if k == 0:
+                occ_copy(other, 0, me).wait_recv()
+            signs(k, lambda offset, up: occ_copy(other + offset, 0, me).wait_recv())
 
     def occ_join():
         for w in range(n):
@@ -299,8 +304,8 @@
         return base + 4 * (plane - z)
 
     def turns(line_base, other_base):
-        order = sorted([(k, 0, line_base) for k in range(nz)] + [(k + 1.5, 1, other_base) for k in range(nz)], key=lambda e: e[:2])
-        return [near(base, int(k - 1.5 * side)) for k, side, base in order]
+        order = sorted([(k, 0, line_base) for k in range(nz)] + [(k + 0.75, 1, other_base) for k in range(nz)], key=lambda e: e[:2])
+        return [near(base, int(k - 0.75 * side)) for k, side, base in order]
 
     def x_relay(count):
         for w in relays[count[0]:count[1]]:
@@ -367,15 +372,32 @@
             @pl.when(jnp.logical_not(far))
             def _():
                 out_ref[w] = total[:, :wide]
-        for w in groups_of[g]:
-            pl.when(far)(lambda: o_copy(w).start())
+        @pl.when(far)
+        def _():
+            for w in groups_of[g]:
+                o_copy(w).start()
+            for slot, packed in slots(groups_of, g):
+                t_out[slot] = sum(pltpu.roll(y_sum[w, :, full * LANES:], j * rest, 1) if j else y_sum[w, :, full * LANES:] for j, w in enumerate(packed))
+                t_copy(slot).start()
+
+    def slots(groups, g):
+        fit = LANES // rest
+        base = sum(-(-len(group) // fit) for group in groups[:g])
+        return [(base + k // fit, groups[g][k:k + fit]) for k in range(0, len(groups[g]), fit)]
+
+    theirs = [turns(xp, diag)] + [turns(me, yp)[k:k + split_at] for k in range(0, n // 2, split_at)]
 
     def last(g):
-        for w in groups_of[g]:
-            @pl.when(far)
-            def _():
+        @pl.when(far)
+        def _():
+            for w in theirs[g]:
                 o_copy(w).wait_recv()
-                out_ref[w] = y_recv[w, :, :wide]
+                out_ref[w, :, :full * LANES] = y_recv[w, :, :full * LANES]
+            for slot, packed in slots(theirs, g):
+                t_copy(slot).wait_recv()
+                tile = t_in[slot]
+                for j, w in enumerate(packed):
+                    out_ref[w, :, full * LANES:] = (pltpu.roll(tile, LANES - j * rest, 1) if j else tile)[:, :rest]
 
     pieces = range(len(parts))
     occ_start()
@@ -389,34 +411,30 @@
         line(1, p, 0)
     for p in pieces:
         turn(0, p)
-    occ_wait()
+    occ_wait(0)
+    occ_wait(1)
+    occ_wait(2)
+    for p in pieces:
+        line(1, p, 1)
+    occ_wait(3)
     occ_join()
     x_other()
+    for p in pieces:
+        line(2, p, 0, over=False)
     x_mine()
-    for p in pieces:
-        line(1, p, 1, over=False)
-    for p in pieces:
-        line(2, p, 0, over=False)
     x_start()
     for p in pieces:
-        line(1, p, 1, on=False)
-    for p in pieces:
         line(2, p, 0, on=False)
     for p in pieces:
         turn(1, p)
     for p in pieces:
         line(2, p, 1)
-    x_relay((0, 1))
     for p in pieces:
         line(3, p, 0)
-    for p in pieces:
-        turn(2, p)
-    x_relay((1, 2))
+    x_relay((0, 4))
     for p in pieces:
         line(3, p, 1)
-    for p in pieces:
-        turn(3, p)
-    x_relay((2, 2 * nz - 1))
+    x_relay((4, 2 * nz - 1))
     join_side(True)
     for p in pieces:
         y_wait(p)
@@ -446,7 +464,9 @@
     for w in range(n):
         y_copy(w).wait_send()
         pl.when(far)(lambda: o_copy(w).wait_send())
-    for g in list(range(1, len(groups_of))) + [0]:
+    for g in range(len(theirs)):
+        for slot, packed in slots(groups_of, g):
+            pl.when(far)(lambda: t_copy(slot).wait_send())
         last(g)
 
 
@@ -498,8 +518,9 @@
             pltpu.VMEM((n // 2, 2 * iblock, tall), F32),
             pltpu.VMEM((n, 2 * iblock, tall), F32),
             *[pltpu.VMEM((n, iblock, spread), F32)] * 4,
+            *[pltpu.VMEM((n, 8, LANES), F32)] * 2,
             dma, dma((nz,)), dma((3, n)), dma((n,)), dma((len(parts),)), dma((3, len(parts), n)), dma((len(parts), n)),
-            dma((n // 2,)), dma((n,)), dma((n,)), dma, dma, *[dma((n,))] * 4,
+            dma((n // 2,)), dma((n,)), dma((n,)), dma, dma, *[dma((n,))] * 6,
         ],
         compiler_params=pltpu.CompilerParams(
             collective_id=0, has_side_effects=True, vmem_limit_bytes=53 * 1024 * 1024),

time: 40.9 us -> 39.4 us (0.963)
  Pallas kernels: 39.1 us -> 37.6 us
    pallas_call x1, Pallas kernels: 39.1 us -> 37.6 us  [body(): pl.pallas_call(functools.partial(kernel, n, starts, rows, deep, sub, part...]
where the time goes in v3:
time: 39.4 us; the launch traced here: 39.3 us
  Pallas kernels  37.6 us (95%)
  local copies, waits for them, and re-layouts  1.65 us (4%)
    pallas_call x1, Pallas kernels, body(): pl.pallas_call(functools.partial(kernel, n, starts, rows, deep, sub, part...  37.6 us
    unnamed x3, local copies, waits for them, and re-layouts  1.65 us

profile of v3, /device:TPU:1, one launch (start us, length us, event | category | flops | bytes accessed | tf_op | source)
XLA Modules:
  0.0 39.3 jit_solution(3210070684445293460)
XLA Ops:
  0.0 0.0 copy-start
  0.0 0.9 %copy-done = f32[1,45000]{1,0:T(1,128)S(1)} copy-done((f32[1,45000]{1,0:T(1,128)S(1)}, f32[1,45000]{1,0:T(1,128)}, u32[]{:S(2)}) %copy-start) | copy-done | bytes 180024
  0.9 37.6 %transform.1 = f32[16,8,536]{2,1,0:T(8,128)S(1)} custom-call(f32[1,45000]{1,0:T(1,128)S(1)} %copy-done, f32[600,1200]{1,0:T(8,128)} %bitcast.1), custom_call_target="tpu_custom_call" | custom-call | tf_op jit(solution)/shard_map/transform/pallas_call | solution.py:495
  38.5 0.7 %copy.4 = f32[16,8,536]{2,1,0:T(8,128)} copy(f32[16,8,536]{2,1,0:T(8,128)S(1)} %transform.1) | data formatting | bytes 548864
Async XLA Ops:
  0.0 0.9 %copy-start = (f32[1,45000]{1,0:T(1,128)S(1)}, f32[1,45000]{1,0:T(1,128)}, u32[]{:S(2)}) copy-start(f32[1,45000]{1,0:T(1,128)} %raw_ref.1) | copy-start | bytes 540004

commit v4 on v3

--- a/solution.py
+++ b/solution.py
@@ -324,37 +324,49 @@
             for k in range(max(first, 1), nz):
                 signs(k, lambda offset, up: recv(vir_copy, p, other + offset, 0, me))
 
-    def join(w):
+    early = parts[0][1] // rows
+    edge = early * LANES
+
+    def join(w, first):
         top = starts[w]
-        for t in range(full):
+        for t in range(early) if first else range(early, full):
             dense[top:top + rows, t * LANES:(t + 1) * LANES] += va[w, t * rows:(t + 1) * rows, :]
+        if first:
+            return
         tail = va[w, body_rows:body_rows + 8, :]
         value = jnp.concatenate([pltpu.roll(tail, (LANES - g * rest) % LANES, 1) if g else tail for g in range(groups)], axis=0)
         value = jnp.where(lane < rest, value, 0)
         dense[top:top + rows, full * LANES:(full + 1) * LANES] += value[:rows]
 
-    def join_side(mine_side):
+    def join_side(mine_side, first):
         for yy in range(2):
             @pl.when((y == yy) == mine_side)
             def _():
                 for w in range(n):
                     if (w // 2) % 2 == yy:
-                        join(w)
+                        join(w, first)
 
     far = core != x
 
-    def ready():
-        high, low = split(dense[...])
-        vh[...] = high
-        vl[...] = low
-
-    def chunk(g):
+    def ready(first):
+        where = slice(0, edge) if first else slice(edge, dense.shape[1])
+        high, low = split(dense[:, where])
+        vh[:, where] = high
+        vl[:, where] = low
+
+    def columns_of(g, where):
+        rows_x = jnp.concatenate([x_recv[w] for w in groups_of[g]], axis=0)
+        return product(split(rows_x), (vh[:, where], vl[:, where]))
+
+    def chunk(g, before=None):
         group = groups_of[g]
         for w in group:
             if g:
                 x_pass(w, me).wait_recv()
-        rows_x = jnp.concatenate([x_recv[w] for w in group], axis=0)
-        value = product(split(rows_x), (vh[...], vl[...]))
+        if before is None:
+            value = columns_of(g, slice(0, dense.shape[1]))
+        else:
+            value = jnp.concatenate([before, columns_of(g, slice(edge, dense.shape[1]))], axis=1)
         for j, w in enumerate(group):
             low = value[j * block:j * block + block // 2]
             high = value[j * block + block // 2:(j + 1) * block]
@@ -435,12 +447,17 @@
     for p in pieces:
         line(3, p, 1)
     x_relay((4, 2 * nz - 1))
-    join_side(True)
-    for p in pieces:
+    join_side(True, True)
+    join_side(True, False)
+    y_wait(0)
+    join_side(False, True)
+    ready(True)
+    before = columns_of(0, slice(0, edge))
+    for p in pieces[1:]:
         y_wait(p)
-    join_side(False)
-    ready()
-    chunk(0)
+    join_side(False, False)
+    ready(False)
+    chunk(0, before)
     for g in range(1, len(groups_of)):
         chunk(g)
         finish(g - 1)

time: 39.4 us -> 39.7 us (level)
  no operation moved by 1% of the time
where the time goes in v4:
time: 39.7 us; the launch traced here: 39.6 us
  Pallas kernels  37.9 us (95%)
  local copies, waits for them, and re-layouts  1.65 us (4%)
    pallas_call x1, Pallas kernels, body(): pl.pallas_call(functools.partial(kernel, n, starts, rows, deep, sub, part...  37.9 us
    unnamed x3, local copies, waits for them, and re-layouts  1.65 us

profile of v4, /device:TPU:1, one launch (start us, length us, event | category | flops | bytes accessed | tf_op | source)
XLA Modules:
  0.0 39.6 jit_solution(14438780759957607009)
XLA Ops:
  0.0 0.0 copy-start
  0.0 0.9 %copy-done = f32[1,45000]{1,0:T(1,128)S(1)} copy-done((f32[1,45000]{1,0:T(1,128)S(1)}, f32[1,45000]{1,0:T(1,128)}, u32[]{:S(2)}) %copy-start) | copy-done | bytes 180024
  0.9 37.9 %transform.1 = f32[16,8,536]{2,1,0:T(8,128)S(1)} custom-call(f32[1,45000]{1,0:T(1,128)S(1)} %copy-done, f32[600,1200]{1,0:T(8,128)} %bitcast.1), custom_call_target="tpu_custom_call" | custom-call | tf_op jit(solution)/shard_map/transform/pallas_call | solution.py:512
  38.8 0.7 %copy.4 = f32[16,8,536]{2,1,0:T(8,128)} copy(f32[16,8,536]{2,1,0:T(8,128)S(1)} %transform.1) | data formatting | bytes 548864
Async XLA Ops:
  0.0 0.9 %copy-start = (f32[1,45000]{1,0:T(1,128)S(1)}, f32[1,45000]{1,0:T(1,128)}, u32[]{:S(2)}) copy-start(f32[1,45000]{1,0:T(1,128)} %raw_ref.1) | copy-start | bytes 540004
